TPU v7x, 32 devices: a whole 2x2x4 slice. The times are simulated.
32 devices in a mesh: area: 4 (over z), rank: 8 (over y, x, core).
Axes of the slice: x: 2, y: 2, z: 4, core: 2. Of those that a mesh axis runs over, the one named last changes fastest.
Arguments:
- membrane: float32 [4, 32768], P(None, ('area', 'rank')), may hold values from -6 to 6
- synaptic_trace: float32 [4, 32768], P(None, ('area', 'rank')), may hold values from 0 to 2
- pending: float32 [2, 4, 32768], P(None, None, ('area', 'rank')), may hold values from -6 to 6
- inter_input: float32 [10, 4, 32768], P(None, None, ('area', 'rank')), may hold values from -4 to 4
- ext_spikes: int32 [10, 4, 32768], P(None, None, ('area', 'rank')), may hold values from 0 to 3
- mem_decay: float32 [32768], P(('area', 'rank')), may hold values from 0.6 to 0.95
- trace_decay_factor: float32 [32768], P(('area', 'rank')), may hold values from 0.3 to 0.8
- threshold: float32 [32768], P(('area', 'rank')), may hold values from 0.5 to 1.5
- weight_tiles: bfloat16 [4, 8, 2, 1024, 1024], P('area', 'rank'), may hold values from -0.125 to 0.125
- tile_source: int32 [4, 8, 2], P('area', 'rank'), may hold values from 0 to 7, as said below
- send_amp: bfloat16 [4, 8, 4, 4, 128], P('area', 'rank'), may hold values from -6 to 6
- send_target: int32 [4, 8, 4, 4, 128], P('area', 'rank'), may hold values from 0 to 10239
- send_count: int32 [4, 8, 4, 4], P('area', 'rank'), may hold values from 0 to 128, as said below
Outputs:
- voltage_final: float32 [4, 32768], P(None, ('area', 'rank'))
- trace_final: float32 [4, 32768], P(None, ('area', 'rank'))
- late_traces: bfloat16 [2, 4, 32768], P(None, None, ('area', 'rank'))
- delivered: float32 [10, 4, 32768], P(None, None, ('area', 'rank'))
Inputs may be any that keep to these rules, and one draw needn't show every extreme that they name: For each area a and each k, tile_source[a, :, k] is a permutation of 0 to 7. Entries of a list from slot send_count on are padding.
All inputs are finite; a program needn't handle non-finite values.
Results may differ from a plain program's by a relative error of at most 0.0034.
Values may be sent and summed in bfloat16 or wider, within the bound.
A program may use at most 64 MiB of HBM per device.

v0:
```python
import jax
import jax.numpy as jnp
from jax import lax
from jax.sharding import PartitionSpec as P

STEPS = 10


def collect_sources(frames_stack, tile_source):
    tile_count = tile_source.shape[2]
    gathered = lax.all_gather(frames_stack[None], "rank", axis=0, tiled=True)
    chosen_entries = [
        lax.dynamic_index_in_dim(gathered, tile_source[0, 0, tile_slot], axis=0, keepdims=False)
        for tile_slot in range(tile_count)
    ]
    return jnp.stack(chosen_entries)


def multiply_weight_blocks(frames_stack, weight_tiles, tile_source):
    frames = frames_stack.shape[0]
    trial_count = frames_stack.shape[1]
    block = frames_stack.shape[2]
    selected = collect_sources(frames_stack, tile_source)
    summed = jnp.zeros((frames * trial_count, block), jnp.float32)
    for tile_slot in range(weight_tiles.shape[2]):
        summed = summed + jnp.dot(
            selected[tile_slot].reshape(frames * trial_count, block),
            weight_tiles[0, 0, tile_slot],
            preferred_element_type=jnp.float32,
        )
    return summed.reshape(frames, trial_count, block)


def deliver_local(got_amp, got_target, got_count, trial_count, block):
    width = got_amp.shape[2]
    in_list = jnp.arange(width, dtype=jnp.int32)[None, None, :] < got_count[:, :, None]
    values = jnp.where(in_list, got_amp.astype(jnp.float32), jnp.float32(0.0))
    delay_step = got_target // block
    local_cell = got_target % block
    trial_index = jnp.arange(trial_count, dtype=jnp.int32)[None, :, None]
    flat_index = (delay_step * trial_count + trial_index) * block + local_cell
    result = jnp.zeros((STEPS * trial_count * block,), jnp.float32)
    result = result.at[flat_index.reshape(-1)].add(values.reshape(-1))
    return result.reshape(STEPS, trial_count, block)


def on_device(
    membrane,
    synaptic_trace,
    pending,
    inter_input,
    ext_spikes,
    mem_decay,
    trace_decay_factor,
    threshold,
    weight_tiles,
    tile_source,
    send_amp,
    send_target,
    send_count,
):
    trial_count = membrane.shape[0]
    block = membrane.shape[1]
    got_amp, got_target, got_count = (
        lax.all_to_all(send_amp[0, 0], "area", split_axis=0, concat_axis=0, tiled=True),
        lax.all_to_all(send_target[0, 0], "area", split_axis=0, concat_axis=0, tiled=True),
        lax.all_to_all(send_count[0, 0], "area", split_axis=0, concat_axis=0, tiled=True),
    )
    membrane_voltage = membrane
    synaptic_trace_state = synaptic_trace
    currents = [pending[0], pending[1]] + [None] * (STEPS - 2)
    history = []
    for step_index in range(STEPS):
        drive_now = (
            currents[step_index]
            + inter_input[step_index]
            + 0.25 * ext_spikes[step_index].astype(jnp.float32)
        )
        membrane_voltage = mem_decay * membrane_voltage + drive_now
        spike_flags = jax.nn.sigmoid(4.0 * (membrane_voltage - threshold))
        membrane_voltage = membrane_voltage * (1.0 - spike_flags)
        synaptic_trace_state = trace_decay_factor * synaptic_trace_state + spike_flags
        sent_trace = synaptic_trace_state.astype(jnp.bfloat16)
        history.append(sent_trace)
        if step_index % 2 == 1 and step_index + 1 < STEPS:
            both_frames = jnp.stack([history[step_index - 1], sent_trace])
            produced = multiply_weight_blocks(both_frames, weight_tiles, tile_source)
            currents[step_index + 1] = produced[0]
            currents[step_index + 2] = produced[1]
    late_traces = jnp.stack([history[STEPS - 2], history[STEPS - 1]])
    delivered = deliver_local(got_amp, got_target, got_count, trial_count, block)
    return (membrane_voltage, synaptic_trace_state, late_traces, delivered)


def solution(mesh):
    placed = (
        P(None, ("area", "rank")),
        P(None, ("area", "rank")),
        P(None, None, ("area", "rank")),
        P(None, None, ("area", "rank")),
        P(None, None, ("area", "rank")),
        P(("area", "rank")),
        P(("area", "rank")),
        P(("area", "rank")),
        P("area", "rank", None, None, None),
        P("area", "rank", None),
        P("area", "rank", None, None, None),
        P("area", "rank", None, None, None),
        P("area", "rank", None, None),
    )
    return jax.shard_map(
        on_device,
        mesh=mesh,
        in_specs=placed,
        out_specs=(
            P(None, ("area", "rank")),
            P(None, ("area", "rank")),
            P(None, None, ("area", "rank")),
            P(None, None, ("area", "rank")),
        ),
        check_vma=False,
    )
```

profile of v0, /device:TPU:0, one launch (start us, length us, event | category | flops | bytes accessed | tf_op | source)
XLA Modules:
  0.0 99.4 jit_solution(6977393147636890913)
XLA Ops:
  0.6 0.0 copy-start
  0.6 0.0 copy-start.1
  0.7 0.0 copy-start.2
  0.7 0.0 copy-start.3
  0.7 0.0 copy-start.4
  0.7 6.5 %all-to-all-start.1 = ((s32[4,1,4]{2,1,0:T(1,128)}), s32[4,1,4]{2,1,0:T(1,128)S(1)}, u32[]{:S(2)}, u32[]{:S(2)}) async-start(s32[4,1,4]{2,1,0:T(1,128)} %bitcast.131), calls=%async_computation.1 | async-start | bytes 4096 | tf_op jit(solution)/shard_map/all_to_all | solution.py:67
  7.2 1.3 %fusion.68 = (s32[1,1,1]{2,1,0:T(1,128)}, s32[1,1,1]{2,1,0:T(1,128)}) fusion(s32[1,1,2]{2,1,0:T(1,128)} %param.22), kind=kLoop, calls=%fused_computation.116 | loop fusion | bytes 16 | tf_op jit(solution)/shard_map/slice | solution.py:13
  11.1 0.9 convert_bitcast_fusion.9
  11.9 0.9 convert_bitcast_fusion.8
  12.8 9.2 %all-gather = bf16[16,4,1024]{2,1,0:T(4,128)(2,1)S(1)} all-gather(bf16[2,4,1024]{2,1,0:T(4,128)(2,1)S(1)} %pad_maximum_fusion), channel_id=2, replica_groups=mesh['area'=4,'rank'=8] {'rank'}, dimensions={0}, use_global_device_ids=true | all-gather | bytes 147456 | tf_op jit(solution)/shard_map/all_gather | solution.py:11
  23.4 2.0 %fusion.6 = f32[8,1024]{1,0:T(8,128)S(1)} fusion(bf16[8,1024]{1,0:T(8,128)(2,1)S(1)} %reshape_squeeze_stack.25, bf16[1,1,2,1024,1024]{4,3,2,1,0:T(8,128)(2,1)} %param.21), kind=kOutput, calls=%fused_computation.7 | convolution fusion | flops 16777216 | bytes 2146304 | tf_op jit(solution)/shard_map/dot_general | solution.py:26
  25.4 2.0 %fusion.24 = f32[8,1024]{1,0:T(8,128)S(1)} fusion(f32[8,1024]{1,0:T(8,128)S(1)} %fusion.6, bf16[8,1024]{1,0:T(8,128)(2,1)S(1)} %reshape_squeeze_stack.24, bf16[1,1,2,1024,1024]{4,3,2,1,0:T(8,128)(2,1)} %param.21), kind=kOutput, calls=%fused_computation.25 | convolution fusion | flops 16785408 | bytes 2179072 | tf_op jit(solution)/shard_map/dot_general | solution.py:26
  27.4 0.0 copy-done
  27.4 0.0 copy-done.1
  27.4 0.0 copy-done.2
  27.4 0.0 copy-done.3
  27.4 0.0 copy-done.4
  27.4 0.1 convert_bitcast_fusion.7
  27.5 0.1 convert_bitcast_fusion.6
  27.6 9.2 %all-gather.1 = bf16[16,4,1024]{2,1,0:T(4,128)(2,1)S(1)} all-gather(bf16[2,4,1024]{2,1,0:T(4,128)(2,1)S(1)} %pad_maximum_fusion.1), channel_id=3, replica_groups=mesh['area'=4,'rank'=8] {'rank'}, dimensions={0}, use_global_device_ids=true | all-gather | bytes 147456 | tf_op jit(solution)/shard_map/all_gather | solution.py:11
  36.8 2.0 %fusion.4 = f32[8,1024]{1,0:T(8,128)S(1)} fusion(bf16[8,1024]{1,0:T(8,128)(2,1)S(1)} %reshape_squeeze_stack.27, bf16[1,1,2,1024,1024]{4,3,2,1,0:T(8,128)(2,1)} %param.21), kind=kOutput, calls=%fused_computation.5 | convolution fusion | flops 16777216 | bytes 2146304 | tf_op jit(solution)/shard_map/dot_general | solution.py:26
  38.8 2.0 %fusion.27 = f32[8,1024]{1,0:T(8,128)S(1)} fusion(f32[8,1024]{1,0:T(8,128)S(1)} %fusion.4, bf16[8,1024]{1,0:T(8,128)(2,1)S(1)} %reshape_squeeze_stack.26, bf16[1,1,2,1024,1024]{4,3,2,1,0:T(8,128)(2,1)} %param.21), kind=kOutput, calls=%fused_computation.26 | convolution fusion | flops 16785408 | bytes 2179072 | tf_op jit(solution)/shard_map/dot_general | solution.py:26
  40.8 0.1 convert_bitcast_fusion.5
  40.8 0.1 convert_bitcast_fusion.4
  40.9 8.2 %all-gather.2 = bf16[16,4,1024]{2,1,0:T(4,128)(2,1)S(1)} all-gather(bf16[2,4,1024]{2,1,0:T(4,128)(2,1)S(1)} %pad_maximum_fusion.2), channel_id=4, replica_groups=mesh['area'=4,'rank'=8] {'rank'}, dimensions={0}, use_global_device_ids=true | all-gather | bytes 147456 | tf_op jit(solution)/shard_map/all_gather | solution.py:11
  49.2 2.0 %fusion.2 = f32[8,1024]{1,0:T(8,128)S(1)} fusion(bf16[8,1024]{1,0:T(8,128)(2,1)S(1)} %reshape_squeeze_stack.29, bf16[1,1,2,1024,1024]{4,3,2,1,0:T(8,128)(2,1)} %param.21), kind=kOutput, calls=%fused_computation.3 | convolution fusion | flops 16777216 | bytes 2146304 | tf_op jit(solution)/shard_map/dot_general | solution.py:26
  51.2 2.0 %fusion.30 = f32[8,1024]{1,0:T(8,128)S(1)} fusion(f32[8,1024]{1,0:T(8,128)S(1)} %fusion.2, bf16[8,1024]{1,0:T(8,128)(2,1)S(1)} %reshape_squeeze_stack.28, bf16[1,1,2,1024,1024]{4,3,2,1,0:T(8,128)(2,1)} %param.21), kind=kOutput, calls=%fused_computation.27 | convolution fusion | flops 16785408 | bytes 2179072 | tf_op jit(solution)/shard_map/dot_general | solution.py:26
  53.1 0.1 convert_bitcast_fusion.3
  53.2 0.1 convert_bitcast_fusion.2
  53.3 9.2 %all-gather.3 = bf16[16,4,1024]{2,1,0:T(4,128)(2,1)S(1)} all-gather(bf16[2,4,1024]{2,1,0:T(4,128)(2,1)S(1)} %pad_maximum_fusion.3), channel_id=5, replica_groups=mesh['area'=4,'rank'=8] {'rank'}, dimensions={0}, use_global_device_ids=true | all-gather | bytes 147456 | tf_op jit(solution)/shard_map/all_gather | solution.py:11
  62.5 2.0 %fusion = f32[8,1024]{1,0:T(8,128)S(1)} fusion(bf16[8,1024]{1,0:T(8,128)(2,1)S(1)} %reshape_squeeze_stack.31, bf16[1,1,2,1024,1024]{4,3,2,1,0:T(8,128)(2,1)} %param.21), kind=kOutput, calls=%fused_computation.1 | convolution fusion | flops 16777216 | bytes 2146304 | tf_op jit(solution)/shard_map/dot_general | solution.py:26
  64.5 2.0 %fusion.33 = f32[8,1024]{1,0:T(8,128)S(1)} fusion(f32[8,1024]{1,0:T(8,128)S(1)} %fusion, bf16[8,1024]{1,0:T(8,128)(2,1)S(1)} %reshape_squeeze_stack.30, bf16[1,1,2,1024,1024]{4,3,2,1,0:T(8,128)(2,1)} %param.21), kind=kOutput, calls=%fused_computation.28 | convolution fusion | flops 16785408 | bytes 2179072 | tf_op jit(solution)/shard_map/dot_general | solution.py:26
  66.5 0.1 convert_bitcast_fusion.1
  66.5 0.7 convert_bitcast_fusion
  67.2 0.6 subtract_multiply_fusion
  67.8 0.0 all-to-all-done.1
  67.8 5.1 %all-to-all-start.2 = ((bf16[4,4,128]{2,1,0:T(4,128)(2,1)}), bf16[4,4,128]{2,1,0:T(4,128)(2,1)S(1)}, u32[]{:S(2)}, u32[]{:S(2)}) async-start(bf16[4,4,128]{2,1,0:T(4,128)(2,1)} %bitcast.42), calls=%async_computation.2 | async-start | bytes 8192 | tf_op jit(solution)/shard_map/all_to_all | solution.py:65
  72.9 0.6 pad_maximum_fusion.4
  73.6 5.0 %all-to-all-done.2 = bf16[4,4,128]{2,1,0:T(4,128)(2,1)S(1)} async-done(((bf16[4,4,128]{2,1,0:T(4,128)(2,1)}), bf16[4,4,128]{2,1,0:T(4,128)(2,1)S(1)}, u32[]{:S(2)}, u32[]{:S(2)}) %all-to-all-start.2) | async-done | bytes 4128 | tf_op jit(solution)/shard_map/all_to_all | solution.py:65
  78.5 3.2 %all-to-all-start = ((s32[4,4,128]{2,1,0:T(4,128)}), s32[4,4,128]{2,1,0:T(4,128)S(1)}, u32[]{:S(2)}, u32[]{:S(2)}) async-start(s32[4,4,128]{2,1,0:T(4,128)} %bitcast.36), calls=%async_computation | async-start | bytes 16384 | tf_op jit(solution)/shard_map/all_to_all | solution.py:66
  81.8 0.1 convert_select_fusion
  81.8 5.5 %all-to-all-done = s32[4,4,128]{2,1,0:T(4,128)S(1)} async-done(((s32[4,4,128]{2,1,0:T(4,128)}), s32[4,4,128]{2,1,0:T(4,128)S(1)}, u32[]{:S(2)}, u32[]{:S(2)}) %all-to-all-start) | async-done | bytes 8224 | tf_op jit(solution)/shard_map/all_to_all | solution.py:66
  87.4 11.3 %scatter_custom_fusion = f32[40960]{0:T(1024)S(1)} fusion(s32[2048]{0:T(1024)S(1)} %bitcast.130, f32[2048]{0:T(1024)S(1)} %bitcast.128, f32[]{:T(128)} %constant.54.clone.1), kind=kCustom, calls=%fused_computation.29 | custom fusion | flops 2048 | bytes 163844 | tf_op jit(solution)/shard_map/scatter-add | solution.py:43
  98.7 0.7 reshape.117
  (18 shorter events, 0.3 us)
Async XLA Ops:
  0.6 26.7 %copy-start = (f32[1024]{0:T(1024)S(1)}, f32[1024]{0:T(1024)}, u32[]{:S(2)}) copy-start(f32[1024]{0:T(1024)} %param.20) | copy-start | bytes 12292
  0.6 26.7 %copy-start.1 = (f32[1024]{0:T(1024)S(1)}, f32[1024]{0:T(1024)}, u32[]{:S(2)}) copy-start(f32[1024]{0:T(1024)} %param.19) | copy-start | bytes 12292
  0.7 26.7 %copy-start.2 = (f32[1024]{0:T(1024)S(1)}, f32[1024]{0:T(1024)}, u32[]{:S(2)}) copy-start(f32[1024]{0:T(1024)} %param.18) | copy-start | bytes 12292
  0.7 26.7 %copy-start.3 = (s32[10,4,1024]{2,1,0:T(4,128)S(1)}, s32[10,4,1024]{2,1,0:T(4,128)}, u32[]{:S(2)}) copy-start(s32[10,4,1024]{2,1,0:T(4,128)} %param.17) | copy-start | bytes 491524
  0.7 26.7 %copy-start.4 = (f32[10,4,1024]{2,1,0:T(4,128)S(1)}, f32[10,4,1024]{2,1,0:T(4,128)}, u32[]{:S(2)}) copy-start(f32[10,4,1024]{2,1,0:T(4,128)} %param.16) | copy-start | bytes 491524
  0.7 67.1 %all-to-all-start.1 = ((s32[4,1,4]{2,1,0:T(1,128)}), s32[4,1,4]{2,1,0:T(1,128)S(1)}, u32[]{:S(2)}, u32[]{:S(2)}) async-start(s32[4,1,4]{2,1,0:T(1,128)} %bitcast.131), calls=%async_computation.1 | async-start | bytes 4096 | tf_op jit(solution)/shard_map/all_to_all | solution.py:67
  67.8 10.7 %all-to-all-start.2 = ((bf16[4,4,128]{2,1,0:T(4,128)(2,1)}), bf16[4,4,128]{2,1,0:T(4,128)(2,1)S(1)}, u32[]{:S(2)}, u32[]{:S(2)}) async-start(bf16[4,4,128]{2,1,0:T(4,128)(2,1)} %bitcast.42), calls=%async_computation.2 | async-start | bytes 8192 | tf_op jit(solution)/shard_map/all_to_all | solution.py:65
  78.5 8.8 %all-to-all-start = ((s32[4,4,128]{2,1,0:T(4,128)}), s32[4,4,128]{2,1,0:T(4,128)S(1)}, u32[]{:S(2)}, u32[]{:S(2)}) async-start(s32[4,4,128]{2,1,0:T(4,128)} %bitcast.36), calls=%async_computation | async-start | bytes 16384 | tf_op jit(solution)/shard_map/all_to_all | solution.py:66
where the time goes:
time: 100 us; the launch traced here: 99.4 us
  blocking collectives  35.8 us (36%)
  matrix products  15.8 us (16%)
  other arithmetic  15.5 us (16%)
  starting transfers between devices  14.8 us (15%)
  waiting for transfers between devices  10.4 us (10%)
  between operations  4.74 us (5%)
  local copies, waits for them, and re-layouts  2.23 us (2%)
    all_gather x4, blocking collectives, collect_sources(): gathered = lax.all_gather(frames_stack[None], 'rank', axis=0, tiled=True)  35.8 us
    dot_general x8, matrix products, multiply_weight_blocks(): jnp.dot(selected[tile_slot].reshape(frames * trial_count, block), weight_...  15.8 us
    scatter-add x1, other arithmetic, deliver_local(): result = result.at[flat_index.reshape(-1)].add(values.reshape(-1))  11.3 us
    all_to_all x1, starting transfers between devices, on_device(): lax.all_to_all(send_count[0, 0], 'area', split_axis=0, concat_axis=0, til...  6.49 us
    all_to_all x1, waiting for transfers between devices, on_device(): lax.all_to_all(send_target[0, 0], 'area', split_axis=0, concat_axis=0, ti...  5.48 us
    all_to_all x1, starting transfers between devices, on_device(): lax.all_to_all(send_amp[0, 0], 'area', split_axis=0, concat_axis=0, tiled...  5.09 us
    all_to_all x1, waiting for transfers between devices, on_device(): lax.all_to_all(send_amp[0, 0], 'area', split_axis=0, concat_axis=0, tiled...  4.96 us
    all_to_all x1, starting transfers between devices, on_device(): lax.all_to_all(send_target[0, 0], 'area', split_axis=0, concat_axis=0, ti...  3.25 us
  transfers between devices with their start and end apart: 3, of which 2 were waited for; matrix products, arithmetic and copies ran while one was open for 22% of the time, Pallas kernels for 0%

commit v1 on v0

v1 whole, which is shorter than its diff:
```python
import functools

import jax
import jax.numpy as jnp
from jax import lax
from jax.experimental import pallas as pl
from jax.experimental.pallas import tpu as pltpu
from jax.sharding import PartitionSpec as P

MESH = pl.DeviceIdType.MESH


def peer_orders(count):
    core = 2 if count % 2 == 0 else 1
    inner = 2 if count % (2 * core) == 0 else 1
    outer = count // (core * inner)
    offsets = [(a, b, c) for a in range(outer) for b in range(inner) for c in range(core)]
    offsets = [o for o in offsets if o != (0, 0, 0)]
    offsets.sort(key=lambda o: -((o[0] != 0) + (o[1] != 0)))
    return (outer, inner, core), offsets


def peer_of(me, sizes, offset):
    outer, inner, core = sizes
    a = (me // (inner * core) + offset[0]) % outer
    b = (me // core % inner + offset[1]) % inner
    c = (me % core + offset[2]) % core
    return (a * inner + b) * core + c


def kernel(areas, ranks, steps, *refs):
    (membrane, trace, pending, inter, ext, decay, trace_decay, threshold, weights, tile_source,
     amp, target, count) = refs[:13]
    voltage_out, trace_out, late_out, delivered_out = refs[13:17]
    (v_in, s_in, pend, inter_v, ext_v, decay_v, td_v, th_v, w_v, src_s, got_amp, got_target, got_count,
     load_sem, send_sem, recv_sem, list_send, list_recv) = refs[17:35]
    frames = refs[35:]
    sends = steps - 2
    trials, block = membrane.shape
    tiles = weights.shape[2]
    rank = lax.axis_index("rank")
    area = lax.axis_index("area")
    sizes, offsets = peer_orders(ranks)

    barrier = pltpu.get_barrier_semaphore()
    for offset in offsets:
        pl.semaphore_signal(barrier, 1, device_id={"rank": peer_of(rank, sizes, offset)}, device_id_type=MESH)
    for shift in range(1, areas):
        pl.semaphore_signal(barrier, 1, device_id={"area": lax.rem(area + shift, areas)}, device_id_type=MESH)

    loads = [
        (membrane, v_in), (trace, s_in), (pending, pend), (inter, inter_v), (ext, ext_v),
        (decay, decay_v), (trace_decay, td_v), (threshold, th_v), (tile_source, src_s),
        (amp.at[0, 0, area], got_amp.at[area]), (target.at[0, 0, area], got_target.at[area]),
        (count.at[0, 0], got_count.at[area]),
    ] + [(weights.at[0, 0, k], w_v.at[pl.ds(k * block, block)]) for k in range(tiles)]
    copies = [pltpu.make_async_copy(a, b, load_sem.at[n]) for n, (a, b) in enumerate(loads)]
    for copy in copies:
        copy.start()
    for copy in copies[:8]:
        copy.wait()

    shape = (trials, block)
    m_decay = jnp.broadcast_to(decay_v[...], shape)
    t_decay = jnp.broadcast_to(td_v[...], shape)
    limit = jnp.broadcast_to(th_v[...], shape)

    def advance(t, v, s, current):
        drive = current + (inter_v[t] + 0.25 * ext_v[t].astype(jnp.float32))
        v = m_decay * v + drive
        firing = 1.0 / (1.0 + jnp.exp(-4.0 * (v - limit)))
        return v * (1.0 - firing), t_decay * s + firing

    def send(t, s):
        frames[t][rank] = s.astype(jnp.bfloat16)
        if t == 0:
            pl.semaphore_wait(barrier, ranks + areas - 2)
        started = []
        for offset in offsets:
            started.append(pltpu.make_async_remote_copy(
                src_ref=frames[t].at[rank], dst_ref=frames[t].at[rank],
                send_sem=send_sem.at[t], recv_sem=recv_sem.at[t],
                device_id={"rank": peer_of(rank, sizes, offset)}, device_id_type=MESH))
        for copy in started:
            copy.start()

    def all_of(t, sem):
        part = frames[t].at[pl.ds(0, ranks - 1)]
        return pltpu.make_async_copy(part, part, sem.at[t])

    v, s = advance(0, v_in[...], s_in[...], pend[0])
    send(0, s)
    lists = []
    for shift in range(1, areas):
        other = lax.rem(area + shift, areas)
        for n, (a, b) in enumerate((
            (amp.at[0, 0, other], got_amp.at[area]), (target.at[0, 0, other], got_target.at[area]),
            (count.at[0, 0], got_count.at[area]),
        )):
            lists.append(pltpu.make_async_remote_copy(
                src_ref=a, dst_ref=b, send_sem=list_send.at[shift, n], recv_sem=list_recv.at[shift, n],
                device_id={"area": other}, device_id_type=MESH))
    v, s = advance(1, v, s, pend[1])
    send(1, s)
    for copy in lists:
        copy.start()
    for copy in copies[8:]:
        copy.wait()
    source = [src_s[0, 0, k] for k in range(tiles)]

    def deliver():
        for copy in lists:
            copy.wait()
        width = got_amp.shape[2]
        lanes = 128
        groups = block // lanes
        rows = groups * steps * trials
        eye = lax.broadcasted_iota(jnp.int32, (trials, trials), 0) == lax.broadcasted_iota(
            jnp.int32, (trials, trials), 1)
        mine = lax.broadcasted_iota(jnp.int32, (areas, trials), 0) == area
        slot = lax.broadcasted_iota(jnp.int32, (trials, width), 1)
        trial = lax.broadcasted_iota(jnp.int32, (trials, width), 0)
        row_id = lax.broadcasted_iota(jnp.int32, (rows, width), 0)
        lane_id = lax.broadcasted_iota(jnp.int32, (lanes, width), 0)
        total = None
        for a in range(areas):
            live = jnp.sum(jnp.where(mine, got_count[a].astype(jnp.float32), 0.0), axis=0, keepdims=True)
            live = jnp.sum(jnp.where(eye, jnp.broadcast_to(live, (trials, trials)), 0.0), axis=1, keepdims=True)
            value = jnp.where(slot < live.astype(jnp.int32), got_amp[a].astype(jnp.float32), 0.0)
            g = got_target[a]
            cell = g % block
            key = (cell // lanes) * (steps * trials) + (g // block) * trials + trial
            low = cell % lanes
            left, right = [], []
            for i in range(trials):
                left.append(jnp.where(row_id == key[i:i + 1], value[i:i + 1], 0.0).astype(jnp.bfloat16))
                right.append(jnp.where(lane_id == low[i:i + 1], 1.0, 0.0).astype(jnp.bfloat16))
            part = lax.dot_general(
                jnp.concatenate(left, axis=1), jnp.concatenate(right, axis=1), (((1,), (1,)), ((), ())),
                preferred_element_type=jnp.float32)
            total = part if total is None else total + part
        for c in range(groups):
            for d in range(steps):
                r = (c * steps + d) * trials
                delivered_out[d, :, c * lanes:(c + 1) * lanes] = total[r:r + trials]

    for t in range(2, steps):
        all_of(t - 2, recv_sem).wait()
        chosen = jnp.concatenate([frames[t - 2][src] for src in source], axis=1)
        current = jnp.dot(chosen, w_v[...], preferred_element_type=jnp.float32)
        v, s = advance(t, v, s, current)
        if t < sends:
            send(t, s)
        else:
            late_out[t - sends] = s.astype(jnp.bfloat16)
        if t == 3:
            deliver()
    voltage_out[...] = v
    trace_out[...] = s
    for t in range(sends):
        all_of(t, send_sem).wait()


def on_device(areas, ranks, *args):
    (membrane, synaptic_trace, pending, inter_input, ext_spikes, mem_decay, trace_decay_factor, threshold,
     weight_tiles, tile_source, send_amp, send_target, send_count) = args
    trials, block = membrane.shape
    steps = inter_input.shape[0]
    tiles = weight_tiles.shape[2]
    width = send_amp.shape[4]
    f32, i32, bf16 = jnp.float32, jnp.int32, jnp.bfloat16
    vmem = pltpu.VMEM
    dma = pltpu.SemaphoreType.DMA
    return pl.pallas_call(
        functools.partial(kernel, areas, ranks, steps),
        out_shape=(
            jax.ShapeDtypeStruct((trials, block), f32),
            jax.ShapeDtypeStruct((trials, block), f32),
            jax.ShapeDtypeStruct((2, trials, block), bf16),
            jax.ShapeDtypeStruct((steps, trials, block), f32),
        ),
        in_specs=[pl.BlockSpec(memory_space=pl.ANY)] * 13,
        out_specs=(pl.BlockSpec(memory_space=pltpu.VMEM),) * 4,
        scratch_shapes=[
            vmem((trials, block), f32), vmem((trials, block), f32), vmem((2, trials, block), f32),
            vmem((steps, trials, block), f32), vmem((steps, trials, block), i32),
            vmem((1, block), f32), vmem((1, block), f32), vmem((1, block), f32),
            vmem((tiles * block, block), bf16), pltpu.SMEM((1, 1, tiles), i32),
            vmem((areas, trials, width), bf16), vmem((areas, trials, width), i32),
            vmem((areas, areas, trials), i32),
            dma((12 + tiles,)), dma((steps - 2,)), dma((steps - 2,)),
            dma((areas, 3)), dma((areas, 3)),
        ] + [vmem((ranks, trials, block), bf16) for _ in range(steps - 2)],
        compiler_params=pltpu.CompilerParams(collective_id=0, has_side_effects=True),
    )(membrane, synaptic_trace, pending, inter_input, ext_spikes, mem_decay.reshape(1, block),
      trace_decay_factor.reshape(1, block), threshold.reshape(1, block), weight_tiles, tile_source,
      send_amp, send_target, send_count)


def solution(mesh):
    both = ("area", "rank")
    placed = (
        P(None, both), P(None, both), P(None, None, both), P(None, None, both), P(None, None, both),
        P(both), P(both), P(both), P("area", "rank", None, None, None), P("area", "rank", None),
        P("area", "rank", None, None, None), P("area", "rank", None, None, None),
        P("area", "rank", None, None),
    )
    return jax.shard_map(
        functools.partial(on_device, mesh.shape["area"], mesh.shape["rank"]),
        mesh=mesh,
        in_specs=placed,
        out_specs=(P(None, both), P(None, both), P(None, None, both), P(None, None, both)),
        check_vma=False,
    )
```

time: 100 us -> 30 us (0.30)
  blocking collectives: 35.8 us -> 0 us
  Pallas kernels: 0 us -> 23.2 us
  matrix products: 15.8 us -> 0 us
  other arithmetic: 15.5 us -> 0 us
  starting transfers between devices: 14.8 us -> 0 us
  waiting for transfers between devices: 10.4 us -> 0 us
  between operations: 4.74 us -> 0.65 us
  local copies, waits for them, and re-layouts: 2.23 us -> 5.57 us
    all_gather x4 -> x0, blocking collectives: 35.8 us -> none  [collect_sources(): gathered = lax.all_gather(frames_stack[None], 'rank', axis=0, tiled=True)]
    pallas_call x0 -> x1, Pallas kernels: none -> 23.2 us  [on_device(): pl.pallas_call(functools.partial(kernel, areas, ranks, steps), out_shape=...]
    dot_general x8 -> x0, matrix products: 15.8 us -> none  [multiply_weight_blocks(): jnp.dot(selected[tile_slot].reshape(frames * trial_count, block), weight_...]
    all_to_all x3 -> x0, starting transfers between devices: 14.8 us -> none  [the longest x1 6.49 us: on_device(): lax.all_to_all(send_count[0, 0], 'area', split_axis=0, concat_axis=0, til...]
    scatter-add x1 -> x0, other arithmetic: 11.3 us -> none  [deliver_local(): result = result.at[flat_index.reshape(-1)].add(values.reshape(-1))]
    all_to_all x3 -> x0, waiting for transfers between devices: 10.4 us -> none  [the longest x1 5.48 us: on_device(): lax.all_to_all(send_target[0, 0], 'area', split_axis=0, concat_axis=0, ti...]
    unnamed x10 -> x4, local copies, waits for them, and re-layouts: 0.03 us -> 5.57 us
    another operation x15 -> x0, other arithmetic: 3.47 us -> none  [the longest x12 2.13 us: on_device(): both_frames = jnp.stack([history[step_index - 1], sent_trace])]
  transfers between devices with their start and end apart: 3 -> 0, of which waited for: 2 -> 0; matrix products, arithmetic and copies ran while one was open for 22% -> 0% of each run, Pallas kernels for 0% -> 0%
where the time goes in v1:
time: 30 us; the launch traced here: 29.4 us
  Pallas kernels  23.2 us (77%)
  local copies, waits for them, and re-layouts  5.57 us (19%)
  between operations  0.65 us (2%)
    pallas_call x1, Pallas kernels, on_device(): pl.pallas_call(functools.partial(kernel, areas, ranks, steps), out_shape=...  23.2 us
    unnamed x4, local copies, waits for them, and re-layouts  5.57 us

profile of v1, /device:TPU:0, one launch (start us, length us, event | category | flops | bytes accessed | tf_op | source)
XLA Modules:
  0.0 29.4 jit_solution(1116826999338040689)
XLA Ops:
  0.6 23.2 %shard_map.156 = (f32[4,1024]{1,0:T(4,128)}, f32[4,1024]{1,0:T(4,128)}, bf16[2,4,1024]{2,1,0:T(4,128)(2,1)}, f32[10,4,1024]{2,1,0:T(4,128)}) custom-call(f32[4,1024]{1,0:T(4,128)} %refs_0_.1, f32[4,1024]{1,0:T(4,128)} %refs_1_.1, f32[2,4,1024]{2,1,0:T(4,128)} %refs_2_.1, f32[10,4,1024]{2,1,0:T(4,128)} %refs_3_.1, s32[10,4,1024]{2,1,0:T(4,128)} %refs_4_.1, ...), custom_call_target="tpu_custom_call" | custom-call | tf_op jit(solution)/shard_map/pallas_call | solution.py:174
  23.8 1.3 %copy.21 = f32[4,1024]{1,0:T(4,128)} copy(f32[4,1024]{1,0:T(4,128)} %get-tuple-element.8) | data formatting | bytes 32768
  25.2 1.3 %copy.22 = f32[4,1024]{1,0:T(4,128)} copy(f32[4,1024]{1,0:T(4,128)} %get-tuple-element.9) | data formatting | bytes 32768
  26.5 1.3 %copy.23 = bf16[2,4,1024]{2,1,0:T(4,128)(2,1)} copy(bf16[2,4,1024]{2,1,0:T(4,128)(2,1)} %get-tuple-element.10) | data formatting | bytes 32768
  27.8 1.6 %copy.24 = f32[10,4,1024]{2,1,0:T(4,128)} copy(f32[10,4,1024]{2,1,0:T(4,128)} %get-tuple-element.11) | data formatting | bytes 327680

commit v2 on v1

--- a/solution.py
+++ b/solution.py
@@ -161,6 +161,15 @@
         all_of(t, send_sem).wait()
 
 
+def hand_over(*refs):
+    sems = refs[8]
+    copies = [pltpu.make_async_copy(refs[n], refs[4 + n], sems.at[n]) for n in range(4)]
+    for copy in copies:
+        copy.start()
+    for copy in copies:
+        copy.wait()
+
+
 def on_device(areas, ranks, *args):
     (membrane, synaptic_trace, pending, inter_input, ext_spikes, mem_decay, trace_decay_factor, threshold,
      weight_tiles, tile_source, send_amp, send_target, send_count) = args
@@ -171,15 +180,16 @@
     f32, i32, bf16 = jnp.float32, jnp.int32, jnp.bfloat16
     vmem = pltpu.VMEM
     dma = pltpu.SemaphoreType.DMA
-    return pl.pallas_call(
+    shapes = (
+        jax.ShapeDtypeStruct((trials, block), f32),
+        jax.ShapeDtypeStruct((trials, block), f32),
+        jax.ShapeDtypeStruct((2, trials, block), bf16),
+        jax.ShapeDtypeStruct((steps, trials, block), f32),
+    )
+    results = pl.pallas_call(
         functools.partial(kernel, areas, ranks, steps),
-        out_shape=(
-            jax.ShapeDtypeStruct((trials, block), f32),
-            jax.ShapeDtypeStruct((trials, block), f32),
-            jax.ShapeDtypeStruct((2, trials, block), bf16),
-            jax.ShapeDtypeStruct((steps, trials, block), f32),
-        ),
-        in_specs=[pl.BlockSpec(memory_space=pl.ANY)] * 13,
+        out_shape=tuple(vmem(x.shape, x.dtype) for x in shapes),
+        in_specs=[pl.BlockSpec(memory_space=pltpu.HBM)] * 13,
         out_specs=(pl.BlockSpec(memory_space=pltpu.VMEM),) * 4,
         scratch_shapes=[
             vmem((trials, block), f32), vmem((trials, block), f32), vmem((2, trials, block), f32),
@@ -195,6 +205,14 @@
     )(membrane, synaptic_trace, pending, inter_input, ext_spikes, mem_decay.reshape(1, block),
       trace_decay_factor.reshape(1, block), threshold.reshape(1, block), weight_tiles, tile_source,
       send_amp, send_target, send_count)
+    return pl.pallas_call(
+        hand_over,
+        out_shape=shapes,
+        in_specs=[pl.BlockSpec(memory_space=pl.ANY)] * 4,
+        out_specs=(pl.BlockSpec(memory_space=pltpu.HBM),) * 4,
+        scratch_shapes=[dma((4,))],
+        compiler_params=pltpu.CompilerParams(vmem_limit_bytes=1 << 20),
+    )(*results)
 
 
 def solution(mesh):

time: 30 us -> 24.1 us (0.80); the launches traced: 29.4 us -> 23.9 us
  local copies, waits for them, and re-layouts: 5.57 us -> 0 us
    unnamed x4 -> x0, local copies, waits for them, and re-layouts: 5.57 us -> none
    pallas_call x0 -> x1, Pallas kernels: none -> 0.72 us  [on_device(): pl.pallas_call(hand_over, out_shape=shapes, in_specs=[pl.BlockSpec(memory...]
    pallas_call x1, Pallas kernels: 23.2 us -> 22.5 us  [on_device(): pl.pallas_call(functools.partial(kernel, areas, ranks, steps), out_shape=...]
where the time goes in v2:
time: 24.1 us; the launch traced here: 23.9 us
  Pallas kernels  23.2 us (96%)
  between operations  0.64 us (3%)
    pallas_call x1, Pallas kernels, on_device(): pl.pallas_call(functools.partial(kernel, areas, ranks, steps), out_shape=...  22.5 us
    pallas_call x1, Pallas kernels, on_device(): pl.pallas_call(hand_over, out_shape=shapes, in_specs=[pl.BlockSpec(memory...  0.72 us

profile of v2, /device:TPU:0, one launch (start us, length us, event | category | flops | bytes accessed | tf_op | source)
XLA Modules:
  0.0 23.9 jit_solution(978889715146826611)
XLA Ops:
  0.6 22.5 %shard_map.156 = (f32[4,1024]{1,0:T(4,128)S(1)}, f32[4,1024]{1,0:T(4,128)S(1)}, bf16[2,4,1024]{2,1,0:T(4,128)(2,1)S(1)}, f32[10,4,1024]{2,1,0:T(4,128)S(1)}) custom-call(f32[4,1024]{1,0:T(4,128)} %refs_0_.1, f32[4,1024]{1,0:T(4,128)} %refs_1_.1, f32[2,4,1024]{2,1,0:T(4,128)} %refs_2_.1, f32[10,4,1024]{2,1,0:T(4,128)} %refs_3_.1, s32[10,4,1024]{2,1,0:T(4,128)} %refs_4_.1, ...), custom_call_target="tpu_custom_call" | custom-call | tf_op jit(solution)/shard_map/pallas_call | solution.py:189
  23.1 0.7 %shard_map.157 = (f32[4,1024]{1,0:T(4,128)}, f32[4,1024]{1,0:T(4,128)}, bf16[2,4,1024]{2,1,0:T(4,128)(2,1)}, f32[10,4,1024]{2,1,0:T(4,128)}) custom-call(f32[4,1024]{1,0:T(4,128)S(1)} %get-tuple-element.8.refs_0_, f32[4,1024]{1,0:T(4,128)S(1)} %get-tuple-element.9.refs_1_, bf16[2,4,1024]{2,1,0:T(4,128)(2,1)S(1)} %get-tuple-element.10.refs_2_, ...), custom_call_target="tpu_custom_call" | custom-call | tf_op jit(solution)/shard_map/pallas_call | solution.py:208

commit v3 on v2

--- a/solution.py
+++ b/solution.py
@@ -45,13 +45,16 @@
     barrier = pltpu.get_barrier_semaphore()
     for offset in offsets:
         pl.semaphore_signal(barrier, 1, device_id={"rank": peer_of(rank, sizes, offset)}, device_id_type=MESH)
-    for shift in range(1, areas):
-        pl.semaphore_signal(barrier, 1, device_id={"area": lax.rem(area + shift, areas)}, device_id_type=MESH)
+    for near in (-1, 1):
+        @pl.when((area + near >= 0) & (area + near < areas))
+        def _():
+            pl.semaphore_signal(barrier, 1, device_id={"area": (area + near + areas) % areas}, device_id_type=MESH)
+    neighbours = (area + areas - 1) // areas + (2 * areas - 2 - area) // areas
 
     loads = [
         (membrane, v_in), (trace, s_in), (pending, pend), (inter, inter_v), (ext, ext_v),
         (decay, decay_v), (trace_decay, td_v), (threshold, th_v), (tile_source, src_s),
-        (amp.at[0, 0, area], got_amp.at[area]), (target.at[0, 0, area], got_target.at[area]),
+        (amp.at[0, 0], got_amp.at[area]), (target.at[0, 0], got_target.at[area]),
         (count.at[0, 0], got_count.at[area]),
     ] + [(weights.at[0, 0, k], w_v.at[pl.ds(k * block, block)]) for k in range(tiles)]
     copies = [pltpu.make_async_copy(a, b, load_sem.at[n]) for n, (a, b) in enumerate(loads)]
@@ -74,7 +77,7 @@
     def send(t, s):
         frames[t][rank] = s.astype(jnp.bfloat16)
         if t == 0:
-            pl.semaphore_wait(barrier, ranks + areas - 2)
+            pl.semaphore_wait(barrier, ranks - 1 + neighbours)
         started = []
         for offset in offsets:
             started.append(pltpu.make_async_remote_copy(
@@ -90,28 +93,45 @@
 
     v, s = advance(0, v_in[...], s_in[...], pend[0])
     send(0, s)
-    lists = []
-    for shift in range(1, areas):
-        other = lax.rem(area + shift, areas)
-        for n, (a, b) in enumerate((
-            (amp.at[0, 0, other], got_amp.at[area]), (target.at[0, 0, other], got_target.at[area]),
-            (count.at[0, 0], got_count.at[area]),
-        )):
-            lists.append(pltpu.make_async_remote_copy(
-                src_ref=a, dst_ref=b, send_sem=list_send.at[shift, n], recv_sem=list_recv.at[shift, n],
-                device_id={"area": other}, device_id_type=MESH))
     v, s = advance(1, v, s, pend[1])
     send(1, s)
-    for copy in lists:
-        copy.start()
     for copy in copies[8:]:
         copy.wait()
     source = [src_s[0, 0, k] for k in range(tiles)]
 
+    def passing(owner, near):
+        other = (area + near + areas) % areas
+        return [pltpu.make_async_remote_copy(
+            src_ref=box.at[owner], dst_ref=box.at[owner], send_sem=list_send.at[owner, (1 - near) // 2, n],
+            recv_sem=list_recv.at[owner, n], device_id={"area": other}, device_id_type=MESH)
+            for n, box in enumerate((got_amp, got_target, got_count))]
+
+    def hop(distance, act):
+        for near in (-1, 1):
+            owner = area - near * (distance - 1)
+            inside = (owner >= 0) & (owner < areas) & (area + near >= 0) & (area + near < areas)
+
+            @pl.when(inside)
+            def _():
+                for copy in passing((owner + areas) % areas, near):
+                    act(copy)
+
+    def arrived(distance):
+        for near in (-1, 1):
+            owner = area - near * distance
+
+            @pl.when((owner >= 0) & (owner < areas))
+            def _():
+                for copy in passing((owner + areas) % areas, near):
+                    copy.wait_recv()
+
+    def exchange(distance):
+        if distance > 1:
+            arrived(distance - 1)
+        hop(distance, lambda copy: copy.start())
+
     def deliver():
-        for copy in lists:
-            copy.wait()
-        width = got_amp.shape[2]
+        width = got_amp.shape[3]
         lanes = 128
         groups = block // lanes
         rows = groups * steps * trials
@@ -126,8 +146,8 @@
         for a in range(areas):
             live = jnp.sum(jnp.where(mine, got_count[a].astype(jnp.float32), 0.0), axis=0, keepdims=True)
             live = jnp.sum(jnp.where(eye, jnp.broadcast_to(live, (trials, trials)), 0.0), axis=1, keepdims=True)
-            value = jnp.where(slot < live.astype(jnp.int32), got_amp[a].astype(jnp.float32), 0.0)
-            g = got_target[a]
+            value = jnp.where(slot < live.astype(jnp.int32), got_amp[a, area].astype(jnp.float32), 0.0)
+            g = got_target[a, area]
             cell = g % block
             key = (cell // lanes) * (steps * trials) + (g // block) * trials + trial
             low = cell % lanes
@@ -144,6 +164,7 @@
                 r = (c * steps + d) * trials
                 delivered_out[d, :, c * lanes:(c + 1) * lanes] = total[r:r + trials]
 
+    exchange(1)
     for t in range(2, steps):
         all_of(t - 2, recv_sem).wait()
         chosen = jnp.concatenate([frames[t - 2][src] for src in source], axis=1)
@@ -153,12 +174,19 @@
             send(t, s)
         else:
             late_out[t - sends] = s.astype(jnp.bfloat16)
-        if t == 3:
+        if t < steps - 3 and t < areas:
+            exchange(t)
+        if t == steps - 4:
+            for distance in range(steps - 3, areas):
+                exchange(distance)
+            arrived(areas - 1)
             deliver()
     voltage_out[...] = v
     trace_out[...] = s
     for t in range(sends):
         all_of(t, send_sem).wait()
+    for distance in range(1, areas):
+        hop(distance, lambda copy: copy.wait_send())
 
 
 def hand_over(*refs):
@@ -196,10 +224,10 @@
             vmem((steps, trials, block), f32), vmem((steps, trials, block), i32),
             vmem((1, block), f32), vmem((1, block), f32), vmem((1, block), f32),
             vmem((tiles * block, block), bf16), pltpu.SMEM((1, 1, tiles), i32),
-            vmem((areas, trials, width), bf16), vmem((areas, trials, width), i32),
+            vmem((areas, areas, trials, width), bf16), vmem((areas, areas, trials, width), i32),
             vmem((areas, areas, trials), i32),
             dma((12 + tiles,)), dma((steps - 2,)), dma((steps - 2,)),
-            dma((areas, 3)), dma((areas, 3)),
+            dma((areas, 2, 3)), dma((areas, 3)),
         ] + [vmem((ranks, trials, block), bf16) for _ in range(steps - 2)],
         compiler_params=pltpu.CompilerParams(collective_id=0, has_side_effects=True),
     )(membrane, synaptic_trace, pending, inter_input, ext_spikes, mem_decay.reshape(1, block),

time: 24.1 us -> 23.5 us (0.975)
  Pallas kernels: 23.2 us -> 22.6 us
    pallas_call x1, Pallas kernels: 22.5 us -> 21.9 us  [on_device(): pl.pallas_call(functools.partial(kernel, areas, ranks, steps), out_shape=...]
where the time goes in v3:
time: 23.5 us; the launch traced here: 23.3 us
  Pallas kernels  22.6 us (96%)
  between operations  0.64 us (3%)
    pallas_call x1, Pallas kernels, on_device(): pl.pallas_call(functools.partial(kernel, areas, ranks, steps), out_shape=...  21.9 us
    pallas_call x1, Pallas kernels, on_device(): pl.pallas_call(hand_over, out_shape=shapes, in_specs=[pl.BlockSpec(memory...  0.72 us

profile of v3, /device:TPU:0, one launch (start us, length us, event | category | flops | bytes accessed | tf_op | source)
XLA Modules:
  0.0 23.3 jit_solution(7210873213696683274)
XLA Ops:
  0.6 21.9 %shard_map.156 = (f32[4,1024]{1,0:T(4,128)S(1)}, f32[4,1024]{1,0:T(4,128)S(1)}, bf16[2,4,1024]{2,1,0:T(4,128)(2,1)S(1)}, f32[10,4,1024]{2,1,0:T(4,128)S(1)}) custom-call(f32[4,1024]{1,0:T(4,128)} %refs_0_.1, f32[4,1024]{1,0:T(4,128)} %refs_1_.1, f32[2,4,1024]{2,1,0:T(4,128)} %refs_2_.1, f32[10,4,1024]{2,1,0:T(4,128)} %refs_3_.1, s32[10,4,1024]{2,1,0:T(4,128)} %refs_4_.1, ...), custom_call_target="tpu_custom_call" | custom-call | tf_op jit(solution)/shard_map/pallas_call | solution.py:217
  22.6 0.7 %shard_map.157 = (f32[4,1024]{1,0:T(4,128)}, f32[4,1024]{1,0:T(4,128)}, bf16[2,4,1024]{2,1,0:T(4,128)(2,1)}, f32[10,4,1024]{2,1,0:T(4,128)}) custom-call(f32[4,1024]{1,0:T(4,128)S(1)} %get-tuple-element.8.refs_0_, f32[4,1024]{1,0:T(4,128)S(1)} %get-tuple-element.9.refs_1_, bf16[2,4,1024]{2,1,0:T(4,128)(2,1)S(1)} %get-tuple-element.10.refs_2_, ...), custom_call_target="tpu_custom_call" | custom-call | tf_op jit(solution)/shard_map/pallas_call | solution.py:236

commit v4 on v3

--- a/solution.py
+++ b/solution.py
@@ -24,7 +24,7 @@
     outer, inner, core = sizes
     a = (me // (inner * core) + offset[0]) % outer
     b = (me // core % inner + offset[1]) % inner
-    c = (me % core + offset[2]) % core
+    c = (me % core + offset[2]) % core if offset[:2] == (0, 0) else offset[2]
     return (a * inner + b) * core + c
 
 
@@ -66,13 +66,14 @@
     shape = (trials, block)
     m_decay = jnp.broadcast_to(decay_v[...], shape)
     t_decay = jnp.broadcast_to(td_v[...], shape)
-    limit = jnp.broadcast_to(th_v[...], shape)
+    twice_limit = jnp.broadcast_to(2.0 * th_v[...], shape)
 
     def advance(t, v, s, current):
-        drive = current + (inter_v[t] + 0.25 * ext_v[t].astype(jnp.float32))
-        v = m_decay * v + drive
-        firing = 1.0 / (1.0 + jnp.exp(-4.0 * (v - limit)))
-        return v * (1.0 - firing), t_decay * s + firing
+        kept = m_decay * v + (inter_v[t] + 0.25 * ext_v[t].astype(jnp.float32))
+        faded = t_decay * s + 0.5
+        v = kept + current
+        bend = jnp.tanh(2.0 * v - twice_limit)
+        return v * (0.5 - 0.5 * bend), faded + 0.5 * bend
 
     def send(t, s):
         frames[t][rank] = s.astype(jnp.bfloat16)

time: 23.5 us -> 23.5 us (level)
  no operation moved by 1% of the time
where the time goes in v4:
time: 23.5 us; the launch traced here: 23.3 us
  Pallas kernels  22.6 us (96%)
  between operations  0.64 us (3%)
    pallas_call x1, Pallas kernels, on_device(): pl.pallas_call(functools.partial(kernel, areas, ranks, steps), out_shape=...  21.9 us
    pallas_call x1, Pallas kernels, on_device(): pl.pallas_call(hand_over, out_shape=shapes, in_specs=[pl.BlockSpec(memory...  0.72 us

profile of v4, /device:TPU:0, one launch (start us, length us, event | category | flops | bytes accessed | tf_op | source)
XLA Modules:
  0.0 23.3 jit_solution(15518777374574156912)
XLA Ops:
  0.6 21.9 %shard_map.156 = (f32[4,1024]{1,0:T(4,128)S(1)}, f32[4,1024]{1,0:T(4,128)S(1)}, bf16[2,4,1024]{2,1,0:T(4,128)(2,1)S(1)}, f32[10,4,1024]{2,1,0:T(4,128)S(1)}) custom-call(f32[4,1024]{1,0:T(4,128)} %refs_0_.1, f32[4,1024]{1,0:T(4,128)} %refs_1_.1, f32[2,4,1024]{2,1,0:T(4,128)} %refs_2_.1, f32[10,4,1024]{2,1,0:T(4,128)} %refs_3_.1, s32[10,4,1024]{2,1,0:T(4,128)} %refs_4_.1, ...), custom_call_target="tpu_custom_call" | custom-call | tf_op jit(solution)/shard_map/pallas_call | solution.py:218
  22.5 0.7 %shard_map.157 = (f32[4,1024]{1,0:T(4,128)}, f32[4,1024]{1,0:T(4,128)}, bf16[2,4,1024]{2,1,0:T(4,128)(2,1)}, f32[10,4,1024]{2,1,0:T(4,128)}) custom-call(f32[4,1024]{1,0:T(4,128)S(1)} %get-tuple-element.8.refs_0_, f32[4,1024]{1,0:T(4,128)S(1)} %get-tuple-element.9.refs_1_, bf16[2,4,1024]{2,1,0:T(4,128)(2,1)S(1)} %get-tuple-element.10.refs_2_, ...), custom_call_target="tpu_custom_call" | custom-call | tf_op jit(solution)/shard_map/pallas_call | solution.py:237

commit v5 on v4

--- a/solution.py
+++ b/solution.py
@@ -166,6 +166,7 @@
                 delivered_out[d, :, c * lanes:(c + 1) * lanes] = total[r:r + trials]
 
     exchange(1)
+    reached = 2
     for t in range(2, steps):
         all_of(t - 2, recv_sem).wait()
         chosen = jnp.concatenate([frames[t - 2][src] for src in source], axis=1)
@@ -175,10 +176,11 @@
             send(t, s)
         else:
             late_out[t - sends] = s.astype(jnp.bfloat16)
-        if t < steps - 3 and t < areas:
-            exchange(t)
-        if t == steps - 4:
-            for distance in range(steps - 3, areas):
+        if t % 2 == 1 and t < steps - 3 and reached < areas:
+            exchange(reached)
+            reached += 1
+        if t == steps - 3:
+            for distance in range(reached, areas):
                 exchange(distance)
             arrived(areas - 1)
             deliver()

time: 23.5 us -> 22.3 us (0.949)
  Pallas kernels: 22.6 us -> 21.4 us
    pallas_call x1, Pallas kernels: 21.9 us -> 20.7 us  [on_device(): pl.pallas_call(functools.partial(kernel, areas, ranks, steps), out_shape=...]
where the time goes in v5:
time: 22.3 us; the launch traced here: 22.1 us
  Pallas kernels  21.4 us (96%)
  between operations  0.64 us (3%)
    pallas_call x1, Pallas kernels, on_device(): pl.pallas_call(functools.partial(kernel, areas, ranks, steps), out_shape=...  20.7 us
    pallas_call x1, Pallas kernels, on_device(): pl.pallas_call(hand_over, out_shape=shapes, in_specs=[pl.BlockSpec(memory...  0.72 us

profile of v5, /device:TPU:0, one launch (start us, length us, event | category | flops | bytes accessed | tf_op | source)
XLA Modules:
  0.0 22.1 jit_solution(7515127523404811688)
XLA Ops:
  0.6 20.7 %shard_map.156 = (f32[4,1024]{1,0:T(4,128)S(1)}, f32[4,1024]{1,0:T(4,128)S(1)}, bf16[2,4,1024]{2,1,0:T(4,128)(2,1)S(1)}, f32[10,4,1024]{2,1,0:T(4,128)S(1)}) custom-call(f32[4,1024]{1,0:T(4,128)} %refs_0_.1, f32[4,1024]{1,0:T(4,128)} %refs_1_.1, f32[2,4,1024]{2,1,0:T(4,128)} %refs_2_.1, f32[10,4,1024]{2,1,0:T(4,128)} %refs_3_.1, s32[10,4,1024]{2,1,0:T(4,128)} %refs_4_.1, ...), custom_call_target="tpu_custom_call" | custom-call | tf_op jit(solution)/shard_map/pallas_call | solution.py:220
  21.4 0.7 %shard_map.157 = (f32[4,1024]{1,0:T(4,128)}, f32[4,1024]{1,0:T(4,128)}, bf16[2,4,1024]{2,1,0:T(4,128)(2,1)}, f32[10,4,1024]{2,1,0:T(4,128)}) custom-call(f32[4,1024]{1,0:T(4,128)S(1)} %get-tuple-element.8.refs_0_, f32[4,1024]{1,0:T(4,128)S(1)} %get-tuple-element.9.refs_1_, bf16[2,4,1024]{2,1,0:T(4,128)(2,1)S(1)} %get-tuple-element.10.refs_2_, ...), custom_call_target="tpu_custom_call" | custom-call | tf_op jit(solution)/shard_map/pallas_call | solution.py:239
